TPU v7x, 32 devices: a whole 2x2x4 slice. The times are simulated.
32 devices in a mesh: mem: 8 (over z, x), geo: 4 (over y, core).
Axes of the slice: x: 2, y: 2, z: 4, core: 2. Of those that a mesh axis runs over, the one named last changes fastest.
Arguments:
- control: float32 [8, 32, 48, 384], P('mem', 'geo'), may hold values from -6 to 6
- kappa_table: float32 [16], replicated, may hold values from 0.02 to 0.24
- kappa_index: int32 [48, 384], replicated, may hold values from 0 to 15
- tile_bounds: int32 [5], replicated, may hold values from 0 to 18432, as said below
- filter_bands: float32 [4, 5, 32], replicated, may hold values from -0.3 to 0.3
- perturbation: bfloat16 [2, 8, 32, 18432], P(None, 'mem', None, 'geo'), may hold values from -6 to 6
Outputs:
- increment: float32 [2, 32, 18432], P(None, 'mem', 'geo')
Inputs may be any that keep to these rules, and one draw needn't show every extreme that they name: tile_bounds[0] is 0, tile_bounds[4] is 18432, and the bounds never fall; tile t holds columns tile_bounds[t] to tile_bounds[t + 1] - 1.
All inputs are finite; a program needn't handle non-finite values.
Results may differ from a plain program's by a relative error of at most 0.005.
Values may be sent and summed in bfloat16 or wider, within the bound.
A program may use at most 64 MiB of HBM per device.

v0:
```python
import jax
import jax.numpy as jnp
from jax import lax
from jax.sharding import PartitionSpec as P

ITERS = 10


def neighbours(state):
    east = jnp.concatenate([state[..., 1:, :], state[..., -1:, :]], axis=-2)
    west = jnp.concatenate([state[..., :1, :], state[..., :-1, :]], axis=-2)
    north = jnp.concatenate([state[..., 1:], state[..., -1:]], axis=-1)
    south = jnp.concatenate([state[..., :1], state[..., :-1]], axis=-1)
    return (east, west, north, south)


def face_weights(kappa_field):
    return tuple((0.5 * (kappa_field + other) for other in neighbours(kappa_field)))


def diffuse_step(state, weights):
    east, west, north, south = neighbours(state)
    update = weights[0] * (east - state) + weights[1] * (west - state)
    update = update + weights[2] * (north - state) + weights[3] * (south - state)
    return state + update


def vertical_filter(values, coefficients):
    levels = values.shape[0]
    padded = jnp.pad(values, ((2, 2), (0, 0)))
    result = values
    for offset in range(5):
        result = result + coefficients[offset] * padded[offset : offset + levels]
    return result


def body(control, kappa_table, kappa_index, tile_bounds, filter_bands, perturbation):
    moved_pert = lax.all_to_all(perturbation, "mem", split_axis=2, concat_axis=1, tiled=True)
    kappa_field = jnp.zeros(kappa_index.shape, jnp.float32)
    for entry in range(kappa_table.shape[0]):
        kappa_field = kappa_field + jnp.where(kappa_index == entry, kappa_table[entry], 0.0)
    weights = face_weights(kappa_field)
    state_field = lax.fori_loop(0, ITERS, lambda step, cur: diffuse_step(cur, weights), control)
    flattened = state_field.reshape(state_field.shape[0], state_field.shape[1], -1)
    by_columns = lax.all_to_all(flattened, "geo", split_axis=2, concat_axis=1, tiled=True)
    width = by_columns.shape[2]
    tiles_count = filter_bands.shape[0]
    columns = lax.axis_index("geo") * width + jnp.arange(width, dtype=jnp.int32)
    tile_ids = jnp.sum((columns[None, :] >= tile_bounds[1:-1][:, None]).astype(jnp.int32), axis=0)
    one_hot = (tile_ids[None, :] == jnp.arange(tiles_count, dtype=jnp.int32)[:, None]).astype(
        jnp.float32
    )
    coefficients = jnp.einsum("tkl,tc->klc", filter_bands, one_hot, precision=lax.Precision.HIGHEST)
    filtered = vertical_filter(by_columns[0], coefficients).astype(jnp.bfloat16)
    moved_filtered = lax.all_to_all(filtered[None], "mem", split_axis=1, concat_axis=0, tiled=True)
    return jnp.sum(
        moved_pert.astype(jnp.float32) * moved_filtered.astype(jnp.float32)[None], axis=1
    )


def solution(mesh):
    in_specs = (P("mem", "geo", None, None), P(), P(), P(), P(), P(None, "mem", None, "geo"))
    out_specs = P(None, "mem", "geo")
    return jax.shard_map(body, mesh=mesh, in_specs=in_specs, out_specs=out_specs, check_vma=False)
```

profile of v0, /device:TPU:0, one launch (start us, length us, event | category | flops | bytes accessed | tf_op | source)
XLA Modules:
  0.0 219.2 jit_solution(1623861114880907975)
XLA Ops:
  0.0 1.1 copy.36
  1.1 1.9 fusion.36
  3.0 10.8 %select_add_fusion = f32[48,384]{1,0:T(8,128)S(1)} fusion(s32[48,384]{1,0:T(8,128)} %param.10, f32[]{:T(128)} %bitcast.16, f32[]{:T(128)} %bitcast.15, f32[]{:T(128)} %bitcast.14, f32[]{:T(128)} %bitcast.13, f32[]{:T(128)} %bitcast.12, f32[]{:T(128)} %bitcast.11, f32[]{:T(128)} %bitcast.10, f32[]{:T(128)} %bitcast.9, f32[]{:T(128)} %bitcast.8, f32[]{:T(128)} %bitcast.7, ...), kind=kLoop, calls=%fused_computation.47 | loop fusion | flops 866304 | bytes 147520 | tf_op jit(solution)/shard_map/add | solution.py:41
  14.1 10.9 %fusion.24 = (f32[48,384]{1,0:T(8,128)S(1)}, f32[48,384]{1,0:T(8,128)S(1)}, f32[48,384]{1,0:T(8,128)S(1)}, f32[48,384]{1,0:T(8,128)S(1)}) fusion(f32[48,383]{1,0:T(8,128)S(1)} %get-tuple-element.64, f32[48,1]{1,0:T(8,128)S(1)} %get-tuple-element.62, f32[48,1]{1,0:T(8,128)S(1)} %get-tuple-element.63, f32[48,383]{1,0:T(8,128)S(1)} %get-tuple-element.65, ...), kind=kLoop, calls=%fused_computation.44 | loop fusion | flops 1087488 | bytes 663616 | tf_op jit(solution)/shard_map/mul | solution.py:18
  24.9 10.2 %while.10 = (s32[]{:T(128)}, f32[1,8,48,384]{3,2,1,0:T(8,128)S(1)}, f32[48,384]{1,0:T(8,128)S(1)}, f32[48,384]{1,0:T(8,128)S(1)}, f32[48,384]{1,0:T(8,128)S(1)}, /*index=5*/f32[48,384]{1,0:T(8,128)S(1)}, s32[]{:T(128)}) while((s32[]{:T(128)}, f32[1,8,48,384]{3,2,1,0:T(8,128)S(1)}, f32[48,384]{1,0:T(8,128)S(1)}, f32[48,384]{1,0:T(8,128)S(1)}, ...), condition=%wide.region_1.2_spmd, body=%wide.region_0.1_spmd.sunk | while | flops 2359298 | bytes 8552525 | solution.py:43
  35.2 5.5 %copy.21 = f32[1,8,48,384]{1,3,2,0:T(8,128)} copy(f32[1,8,48,384]{3,2,1,0:T(8,128)S(1)} %get-tuple-element.37) | data formatting | bytes 1179648 | tf_op jit(solution)/shard_map/while | solution.py:43
  41.2 83.6 %reduce.2 = f32[18432,8]{1,0:T(8,128)} reduce(f32[18432,1,8]{2,1,0:T(1,128)} %bitcast.70, f32[]{:T(128)} %broadcast.28), dimensions={1}, to_apply=%bitcast.62.reduce_sub_computation | reduce | bytes 1179652
  124.8 7.8 %reshape.43 = f32[4,1,36864]{2,1,0:T(1,128)} reshape(f32[18432,8]{1,0:T(8,128)} %reduce.2) | data formatting | bytes 1179648
  132.6 4.3 %all-to-all-start.1 = ((f32[4,1,36864]{2,1,0:T(1,128)}), f32[4,1,36864]{2,1,0:T(1,128)}, u32[]{:S(2)}, u32[]{:S(2)}) async-start(f32[4,1,36864]{2,1,0:T(1,128)} %reshape.43), calls=%async_computation.1 | async-start | bytes 1179648 | tf_op jit(solution)/shard_map/all_to_all | solution.py:45
  137.2 1.3 convolution_bitcast_fusion
  138.5 8.5 %all-to-all-done.1 = f32[4,1,36864]{2,1,0:T(1,128)} async-done(((f32[4,1,36864]{2,1,0:T(1,128)}), f32[4,1,36864]{2,1,0:T(1,128)}, u32[]{:S(2)}, u32[]{:S(2)}) %all-to-all-start.1) | async-done | bytes 589856 | tf_op jit(solution)/shard_map/all_to_all | solution.py:45
  147.0 3.3 %reduce.3 = f32[4,36864]{1,0:T(4,128)S(1)} reduce(f32[4,1,36864]{2,1,0:T(1,128)} %all-to-all-done.1, f32[]{:T(128)} %broadcast.28), dimensions={1}, to_apply=%all_to_all.11.reduce_sub_computation | reduce | bytes 1179652 | tf_op jit(solution)/shard_map/all_to_all | solution.py:45
  150.3 22.3 %reshape.44 = f32[18432,1,8]{2,1,0:T(1,128)} reshape(f32[4,36864]{1,0:T(4,128)S(1)} %reduce.3) | data formatting | bytes 1179648
  172.6 5.5 %copy.22 = f32[1,8,4,4608]{3,1,2,0:T(8,128)S(1)} copy(f32[1,8,4,4608]{1,3,2,0:T(8,128)} %bitcast.71) | data formatting | bytes 1179648 | tf_op jit(solution)/shard_map/all_to_all | solution.py:45
  179.5 2.5 %reduce.4 = bf16[32,4608]{1,0:T(8,128)(2,1)S(1)} reduce(bf16[32,1,4608]{2,1,0:T(2,128)(2,1)S(1)} %bitcast.72, bf16[]{:T(256)} %broadcast.30), dimensions={1}, to_apply=%bitcast.69.reduce_sub_computation | reduce | bytes 589826
  181.9 0.9 reshape.45
  182.8 6.6 %all-to-all-start.2 = ((bf16[8,2,9216]{2,1,0:T(2,128)(2,1)}), bf16[8,2,9216]{2,1,0:T(2,128)(2,1)S(1)}, u32[]{:S(2)}, u32[]{:S(2)}) async-start(bf16[8,2,9216]{2,1,0:T(2,128)(2,1)} %reshape.45), calls=%async_computation.2 | async-start | bytes 589824 | tf_op jit(solution)/shard_map/all_to_all | solution.py:55
  189.4 1.4 copy.20
  190.8 7.9 %all-to-all-done.2 = bf16[8,2,9216]{2,1,0:T(2,128)(2,1)S(1)} async-done(((bf16[8,2,9216]{2,1,0:T(2,128)(2,1)}), bf16[8,2,9216]{2,1,0:T(2,128)(2,1)S(1)}, u32[]{:S(2)}, u32[]{:S(2)}) %all-to-all-start.2) | async-done | bytes 294944 | tf_op jit(solution)/shard_map/all_to_all | solution.py:55
  198.7 3.6 %all-to-all-start = ((bf16[2,1,32,4608]{3,0,1,2:T(2,128)(2,1)}), bf16[2,1,32,4608]{3,0,1,2:T(2,128)(2,1)S(1)}, u32[]{:S(2)}, u32[]{:S(2)}) async-start(bf16[2,1,32,4608]{3,0,1,2:T(2,128)(2,1)} %copy.20), calls=%async_computation | async-start | bytes 1179648 | tf_op jit(solution)/shard_map/all_to_all | solution.py:38
  202.6 1.7 convert_reduce_fusion
  204.5 13.4 %all-to-all-done = bf16[2,1,32,4608]{3,0,1,2:T(2,128)(2,1)S(1)} async-done(((bf16[2,1,32,4608]{3,0,1,2:T(2,128)(2,1)}), bf16[2,1,32,4608]{3,0,1,2:T(2,128)(2,1)S(1)}, u32[]{:S(2)}, u32[]{:S(2)}) %all-to-all-start) | async-done | bytes 589856 | tf_op jit(solution)/shard_map/all_to_all | solution.py:38
  217.9 0.6 fusion.8
  218.5 0.7 copy.24
  (69 shorter events, 12.4 us)
Async XLA Ops:
  0.0 137.2 %copy-start = (f32[4,5,32]{2,0,1:T(4,128)S(1)}, f32[4,5,32]{2,0,1:T(4,128)}, u32[]{:S(2)}) copy-start(f32[4,5,32]{2,0,1:T(4,128)} %param.12) | copy-start | bytes 7684
  124.8 12.2 %copy-start.2 = (s32[5]{0:T(128)S(1)}, s32[5]{0:T(128)}, u32[]{:S(2)}) copy-start(s32[5]{0:T(128)} %param.11) | copy-start | bytes 64
  132.6 14.4 %all-to-all-start.1 = ((f32[4,1,36864]{2,1,0:T(1,128)}), f32[4,1,36864]{2,1,0:T(1,128)}, u32[]{:S(2)}, u32[]{:S(2)}) async-start(f32[4,1,36864]{2,1,0:T(1,128)} %reshape.43), calls=%async_computation.1 | async-start | bytes 1179648 | tf_op jit(solution)/shard_map/all_to_all | solution.py:45
  178.5 10.9 %copy-start.1 = (bf16[2,1,32,4608]{3,2,1,0:T(8,128)(2,1)S(1)}, bf16[2,1,32,4608]{3,2,1,0:T(8,128)(2,1)}, u32[]{:S(2)}) copy-start(bf16[2,1,32,4608]{3,2,1,0:T(8,128)(2,1)} %param.13) | copy-start | bytes 1769476
  182.8 15.8 %all-to-all-start.2 = ((bf16[8,2,9216]{2,1,0:T(2,128)(2,1)}), bf16[8,2,9216]{2,1,0:T(2,128)(2,1)S(1)}, u32[]{:S(2)}, u32[]{:S(2)}) async-start(bf16[8,2,9216]{2,1,0:T(2,128)(2,1)} %reshape.45), calls=%async_computation.2 | async-start | bytes 589824 | tf_op jit(solution)/shard_map/all_to_all | solution.py:55
  198.7 19.2 %all-to-all-start = ((bf16[2,1,32,4608]{3,0,1,2:T(2,128)(2,1)}), bf16[2,1,32,4608]{3,0,1,2:T(2,128)(2,1)S(1)}, u32[]{:S(2)}, u32[]{:S(2)}) async-start(bf16[2,1,32,4608]{3,0,1,2:T(2,128)(2,1)} %copy.20), calls=%async_computation | async-start | bytes 1179648 | tf_op jit(solution)/shard_map/all_to_all | solution.py:38
where the time goes:
time: 220 us; the launch traced here: 219 us
  other arithmetic  119 us (54%)
  local copies, waits for them, and re-layouts  53.6 us (24%)
  waiting for transfers between devices  29.8 us (14%)
  starting transfers between devices  14.5 us (7%)
    unnamed x2, other arithmetic  86 us
    unnamed x14, local copies, waits for them, and re-layouts  34.8 us
    all_to_all x1, waiting for transfers between devices, body(): lax.all_to_all(perturbation, 'mem', split_axis=2, concat_axis=1, tiled=True)  13.4 us
    mul x1, other arithmetic, face_weights(): 0.5 * (kappa_field + other)  10.9 us
    add x1, other arithmetic, body(): kappa_field + jnp.where(kappa_index == entry, kappa_table[entry], 0.0)  10.8 us
    all_to_all x1, waiting for transfers between devices, body(): lax.all_to_all(flattened, 'geo', split_axis=2, concat_axis=1, tiled=True)  8.52 us
    all_to_all x1, waiting for transfers between devices, body(): lax.all_to_all(filtered[None], 'mem', split_axis=1, concat_axis=0, tiled=...  7.85 us
    all_to_all x1, starting transfers between devices, body(): lax.all_to_all(filtered[None], 'mem', split_axis=1, concat_axis=0, tiled=...  6.57 us
  transfers between devices with their start and end apart: 3, of which 3 were waited for; matrix products, arithmetic and copies ran while one was open for 2% of the time, Pallas kernels for 0%

commit v1 on v0

--- a/solution.py
+++ b/solution.py
@@ -42,7 +42,21 @@
     weights = face_weights(kappa_field)
     state_field = lax.fori_loop(0, ITERS, lambda step, cur: diffuse_step(cur, weights), control)
     flattened = state_field.reshape(state_field.shape[0], state_field.shape[1], -1)
-    by_columns = lax.all_to_all(flattened, "geo", split_axis=2, concat_axis=1, tiled=True)
+    res = lax.axis_size("geo")
+    local_now, view_out = (res, lax.axis_index("geo"))
+    wide_out = flattened.shape[2] // local_now
+    val = list(flattened.shape)
+    val[2] = wide_out
+    t1 = val[1]
+    val[1] = t1 * local_now
+    by_columns = jnp.zeros(val, flattened.dtype)
+    for num in range(local_now):
+        answer = lax.dynamic_slice_in_dim(flattened, (view_out ^ num) * wide_out, wide_out, axis=2)
+        if num:
+            answer = lax.ppermute(answer, "geo", [(j, j ^ num) for j in range(local_now)])
+        by_columns = lax.dynamic_update_slice_in_dim(
+            by_columns, answer, (view_out ^ num) * t1, axis=1
+        )
     width = by_columns.shape[2]
     tiles_count = filter_bands.shape[0]
     columns = lax.axis_index("geo") * width + jnp.arange(width, dtype=jnp.int32)

time: 220 us -> 90.3 us (0.41)
  other arithmetic: 119 us -> 32.8 us
  local copies, waits for them, and re-layouts: 53.6 us -> 15.7 us
  waiting for transfers between devices: 29.8 us -> 26.6 us
    unnamed x2 -> x1, other arithmetic: 86 us -> 2.45 us
    unnamed x14 -> x11, local copies, waits for them, and re-layouts: 34.8 us -> 4.17 us
    all_to_all x1 -> x0, waiting for transfers between devices: 8.52 us -> none  [body(): lax.all_to_all(flattened, 'geo', split_axis=2, concat_axis=1, tiled=True)]
    while x1 -> x0, local copies, waits for them, and re-layouts: 5.53 us -> none  [body(): lax.fori_loop(0, ITERS, lambda step, cur: diffuse_step(cur, weights), con...]
    all_to_all x1 -> x0, local copies, waits for them, and re-layouts: 5.48 us -> none  [body(): lax.all_to_all(flattened, 'geo', split_axis=2, concat_axis=1, tiled=True)]
    all_to_all x1 -> x0, starting transfers between devices: 4.32 us -> none  [body(): lax.all_to_all(flattened, 'geo', split_axis=2, concat_axis=1, tiled=True)]
    ppermute x0 -> x3, waiting for transfers between devices: none -> 4.16 us  [body(): lax.ppermute(answer, 'geo', [(j, j ^ num) for j in range(local_now)])]
    all_to_all x1 -> x0, other arithmetic: 3.25 us -> none  [body(): lax.all_to_all(flattened, 'geo', split_axis=2, concat_axis=1, tiled=True)]
  transfers between devices with their start and end apart: 3 -> 5, of which waited for: 3 -> 4; matrix products, arithmetic and copies ran while one was open for 2% -> 8% of each run, Pallas kernels for 0% -> 0%
where the time goes in v1:
time: 90.3 us; the launch traced here: 89.5 us
  other arithmetic  32.8 us (36%)
  waiting for transfers between devices  26.6 us (29%)
  local copies, waits for them, and re-layouts  15.7 us (17%)
  starting transfers between devices  12.5 us (14%)
  matrix products  1.34 us (1%)
    all_to_all x1, waiting for transfers between devices, body(): lax.all_to_all(perturbation, 'mem', split_axis=2, concat_axis=1, tiled=True)  13.9 us
    mul x1, other arithmetic, face_weights(): 0.5 * (kappa_field + other)  11 us
    add x1, other arithmetic, body(): kappa_field + jnp.where(kappa_index == entry, kappa_table[entry], 0.0)  11 us
    all_to_all x1, waiting for transfers between devices, body(): lax.all_to_all(filtered[None], 'mem', split_axis=1, concat_axis=0, tiled=...  8.6 us
    all_to_all x1, starting transfers between devices, body(): lax.all_to_all(filtered[None], 'mem', split_axis=1, concat_axis=0, tiled=...  5.75 us
    add x10, other arithmetic, diffuse_step(): return state + update  5.46 us
    unnamed x11, local copies, waits for them, and re-layouts  4.17 us
    ppermute x3, waiting for transfers between devices, body(): lax.ppermute(answer, 'geo', [(j, j ^ num) for j in range(local_now)])  4.16 us
  transfers between devices with their start and end apart: 5, of which 4 were waited for; matrix products, arithmetic and copies ran while one was open for 8% of the time, Pallas kernels for 0%

profile of v1, /device:TPU:0, one launch (start us, length us, event | category | flops | bytes accessed | tf_op | source)
XLA Modules:
  0.0 89.5 jit_solution(14284369988036795165)
XLA Ops:
  0.0 1.1 %copy.31 = f32[1,8,48,384]{3,2,1,0:T(8,128)S(1)} copy(f32[1,8,48,384]{3,2,1,0:T(8,128)} %param.8) | data formatting | bytes 1179648
  1.1 2.0 %fusion.36 = (f32[1]{0:T(128)}, f32[1]{0:T(128)}, f32[1]{0:T(128)}, f32[1]{0:T(128)}, f32[1]{0:T(128)}, /*index=5*/f32[1]{0:T(128)}, f32[1]{0:T(128)}, f32[1]{0:...) fusion(f32[16]{0:T(128)} %param.9), kind=kLoop, calls=%fused_computation.66 | loop fusion | bytes 128 | tf_op jit(solution)/shard_map/slice | solution.py:41
  3.0 11.0 %select_add_fusion = f32[48,384]{1,0:T(8,128)S(1)} fusion(s32[48,384]{1,0:T(8,128)} %param.10, f32[]{:T(128)} %bitcast.16, f32[]{:T(128)} %bitcast.15, f32[]{:T(128)} %bitcast.14, f32[]{:T(128)} %bitcast.13, f32[]{:T(128)} %bitcast.12, f32[]{:T(128)} %bitcast.11, f32[]{:T(128)} %bitcast.10, f32[]{:T(128)} %bitcast.9, f32[]{:T(128)} %bitcast.8, f32[]{:T(128)} %bitcast.7, ...), kind=kLoop, calls=%fused_computation.51 | loop fusion | flops 866304 | bytes 147520 | tf_op jit(solution)/shard_map/add | solution.py:41
  14.2 11.0 %fusion.24 = (f32[48,384]{1,0:T(8,128)S(1)}, f32[48,384]{1,0:T(8,128)S(1)}, f32[48,384]{1,0:T(8,128)S(1)}, f32[48,384]{1,0:T(8,128)S(1)}) fusion(f32[48,383]{1,0:T(8,128)S(1)} %get-tuple-element.67, f32[48,1]{1,0:T(8,128)S(1)} %get-tuple-element.65, f32[48,1]{1,0:T(8,128)S(1)} %get-tuple-element.66, f32[48,383]{1,0:T(8,128)S(1)} %get-tuple-element.68, ...), kind=kLoop, calls=%fused_computation.48 | loop fusion | flops 1087488 | bytes 663616 | tf_op jit(solution)/shard_map/mul | solution.py:18
  25.3 10.2 %while.10 = (s32[]{:T(128)}, f32[1,8,48,384]{3,2,1,0:T(8,128)S(1)}, f32[48,384]{1,0:T(8,128)S(1)}, f32[48,384]{1,0:T(8,128)S(1)}, f32[48,384]{1,0:T(8,128)S(1)}, /*index=5*/f32[48,384]{1,0:T(8,128)S(1)}, s32[]{:T(128)}) while((s32[]{:T(128)}, f32[1,8,48,384]{3,2,1,0:T(8,128)S(1)}, f32[48,384]{1,0:T(8,128)S(1)}, f32[48,384]{1,0:T(8,128)S(1)}, ...), condition=%wide.region_1.2_spmd, body=%wide.region_0.1_spmd.sunk | while | flops 2359298 | bytes 8552525 | solution.py:43
  25.7 0.5 fusion.47
  35.6 0.8 constant_dynamic-slice_fusion
  36.8 2.5 %collective-permute-start.1 = (f32[1,8,4608]{2,1,0:T(8,128)}, f32[1,8,4608]{2,1,0:T(8,128)}, u32[]{:S(2)}, u32[]{:S(2)}) collective-permute-start(f32[1,8,4608]{2,1,0:T(8,128)} %get-tuple-element.59), channel_id=1, source_target_pairs={{0,2},{1,3},{2,0},{3,1},{4,6},{5,7},{6,4},{7,5},{8,10},{9,11},{10,... | collective-permute-start | bytes 442376 | tf_op jit(solution)/shard_map/ppermute | solution.py:56
  39.8 1.3 %convolution_bitcast_fusion = f32[5,32,4608]{2,1,0:T(8,128)S(1)} fusion(f32[4,5,32]{2,0,1:T(4,128)S(1)} %copy-done, s32[4608]{0:T(1024)S(1)} %convert_reduce_fusion.1), kind=kOutput, calls=%fused_computation.12 | convolution fusion | flops 35407872 | bytes 2970112 | tf_op jit(solution)/shard_map/tkl,tc->klc/dot_general | solution.py:67
  41.1 0.9 %bitcast_dynamic-update-slice_fusion.2 = f32[32,4608]{1,0:T(8,128)S(1)} fusion(f32[32,4608]{1,0:T(8,128)S(1)} %bitcast_dynamic-update-slice_fusion.3, s32[]{:T(128)S(6)} %select_n.92, f32[1,8,4608]{2,1,0:T(8,128)} %collective-permute-done), kind=kLoop, calls=%fused_computation.39 | loop fusion | bytes 294916 | tf_op jit(solution)/shard_map/dynamic_update_slice | solution.py:57
  42.1 2.3 %collective-permute-done.1 = f32[1,8,4608]{2,1,0:T(8,128)} collective-permute-done((f32[1,8,4608]{2,1,0:T(8,128)}, f32[1,8,4608]{2,1,0:T(8,128)}, u32[]{:S(2)}, u32[]{:S(2)}) %collective-permute-start.1) | collective-permute-done | bytes 147488 | tf_op jit(solution)/shard_map/ppermute | solution.py:56
  44.4 0.9 %bitcast_dynamic-update-slice_fusion.1 = f32[32,4608]{1,0:T(8,128)S(1)} fusion(f32[32,4608]{1,0:T(8,128)S(1)} %bitcast_dynamic-update-slice_fusion.2, s32[]{:T(128)S(6)} %select_n.94, f32[1,8,4608]{2,1,0:T(8,128)} %collective-permute-done.1), kind=kLoop, calls=%fused_computation.38 | loop fusion | bytes 294916 | tf_op jit(solution)/shard_map/dynamic_update_slice | solution.py:57
  45.3 1.9 %collective-permute-done.2 = f32[1,8,4608]{2,1,0:T(8,128)} collective-permute-done((f32[1,8,4608]{2,1,0:T(8,128)}, f32[1,8,4608]{2,1,0:T(8,128)}, u32[]{:S(2)}, u32[]{:S(2)}) %collective-permute-start.2) | collective-permute-done | bytes 147488 | tf_op jit(solution)/shard_map/ppermute | solution.py:56
  47.2 0.9 %bitcast_dynamic-update-slice_fusion = f32[32,4608]{1,0:T(8,128)S(1)} fusion(f32[32,4608]{1,0:T(8,128)S(1)} %bitcast_dynamic-update-slice_fusion.1, s32[]{:T(128)S(6)} %select_n.96, f32[1,8,4608]{2,1,0:T(8,128)} %collective-permute-done.2), kind=kLoop, calls=%fused_computation.37 | loop fusion | bytes 294916 | tf_op jit(solution)/shard_map/dynamic_update_slice | solution.py:57
  49.4 2.4 %reduce.2 = bf16[32,4608]{1,0:T(8,128)(2,1)S(1)} reduce(bf16[32,1,4608]{2,1,0:T(2,128)(2,1)S(1)} %bitcast.73, bf16[]{:T(256)} %broadcast.30), dimensions={1}, to_apply=%bitcast.72.reduce_sub_computation | reduce | bytes 589826
  51.9 0.9 %reshape.50 = bf16[8,2,9216]{2,1,0:T(2,128)(2,1)} reshape(bf16[32,4608]{1,0:T(8,128)(2,1)S(1)} %reduce.2) | data formatting | bytes 589824
  52.8 5.7 %all-to-all-start.1 = ((bf16[8,2,9216]{2,1,0:T(2,128)(2,1)}), bf16[8,2,9216]{2,1,0:T(2,128)(2,1)S(1)}, u32[]{:S(2)}, u32[]{:S(2)}) async-start(bf16[8,2,9216]{2,1,0:T(2,128)(2,1)} %reshape.50), calls=%async_computation.1 | async-start | bytes 589824 | tf_op jit(solution)/shard_map/all_to_all | solution.py:69
  58.5 1.4 %copy.14 = bf16[2,1,32,4608]{3,0,1,2:T(2,128)(2,1)} copy(bf16[2,1,32,4608]{3,2,1,0:T(8,128)(2,1)S(1)} %copy-done.1) | data formatting | bytes 1179648 | tf_op args[5]
  60.0 8.6 %all-to-all-done.1 = bf16[8,2,9216]{2,1,0:T(2,128)(2,1)S(1)} async-done(((bf16[8,2,9216]{2,1,0:T(2,128)(2,1)}), bf16[8,2,9216]{2,1,0:T(2,128)(2,1)S(1)}, u32[]{:S(2)}, u32[]{:S(2)}) %all-to-all-start.1) | async-done | bytes 294944 | tf_op jit(solution)/shard_map/all_to_all | solution.py:69
  68.6 3.6 %all-to-all-start = ((bf16[2,1,32,4608]{3,0,1,2:T(2,128)(2,1)}), bf16[2,1,32,4608]{3,0,1,2:T(2,128)(2,1)S(1)}, u32[]{:S(2)}, u32[]{:S(2)}) async-start(bf16[2,1,32,4608]{3,0,1,2:T(2,128)(2,1)} %copy.14), calls=%async_computation | async-start | bytes 1179648 | tf_op jit(solution)/shard_map/all_to_all | solution.py:38
  72.5 1.7 %convert_reduce_fusion = f32[32,4608]{1,0:T(8,128)S(1)} fusion(bf16[32,1,4608]{2,1,0:T(2,128)(2,1)S(1)} %reshape.51), kind=kLoop, calls=%fused_computation.35 | loop fusion | flops 147456 | bytes 884736 | tf_op jit(solution)/shard_map/convert_element_type | solution.py:71
  74.3 13.9 %all-to-all-done = bf16[2,1,32,4608]{3,0,1,2:T(2,128)(2,1)S(1)} async-done(((bf16[2,1,32,4608]{3,0,1,2:T(2,128)(2,1)}), bf16[2,1,32,4608]{3,0,1,2:T(2,128)(2,1)S(1)}, u32[]{:S(2)}, u32[]{:S(2)}) %all-to-all-start) | async-done | bytes 589856 | tf_op jit(solution)/shard_map/all_to_all | solution.py:38
  88.2 0.6 fusion.8
  88.8 0.7 copy.16
  (73 shorter events, 12.1 us)
Async XLA Ops:
  0.0 39.7 %copy-start = (f32[4,5,32]{2,0,1:T(4,128)S(1)}, f32[4,5,32]{2,0,1:T(4,128)}, u32[]{:S(2)}) copy-start(f32[4,5,32]{2,0,1:T(4,128)} %param.12) | copy-start | bytes 7684
  25.3 14.2 %copy-start.2 = (s32[5]{0:T(128)S(1)}, s32[5]{0:T(128)}, u32[]{:S(2)}) copy-start(s32[5]{0:T(128)} %param.11) | copy-start | bytes 64
  36.3 4.8 %collective-permute-start = (f32[1,8,4608]{2,1,0:T(8,128)}, f32[1,8,4608]{2,1,0:T(8,128)}, u32[]{:S(2)}, u32[]{:S(2)}) collective-permute-start(f32[1,8,4608]{2,1,0:T(8,128)} %get-tuple-element.60), channel_id=1, source_target_pairs={{0,1},{1,0},{2,3},{3,2},{4,5},{5,4},{6,7},{7,6},{8,9},{9,8},{10,11... | collective-permute-start | bytes 442376 | tf_op jit(solution)/shard_map/ppermute | solution.py:56
  36.8 7.5 %collective-permute-start.1 = (f32[1,8,4608]{2,1,0:T(8,128)}, f32[1,8,4608]{2,1,0:T(8,128)}, u32[]{:S(2)}, u32[]{:S(2)}) collective-permute-start(f32[1,8,4608]{2,1,0:T(8,128)} %get-tuple-element.59), channel_id=1, source_target_pairs={{0,2},{1,3},{2,0},{3,1},{4,6},{5,7},{6,4},{7,5},{8,10},{9,11},{10,... | collective-permute-start | bytes 442376 | tf_op jit(solution)/shard_map/ppermute | solution.py:56
  39.3 7.8 %collective-permute-start.2 = (f32[1,8,4608]{2,1,0:T(8,128)}, f32[1,8,4608]{2,1,0:T(8,128)}, u32[]{:S(2)}, u32[]{:S(2)}) collective-permute-start(f32[1,8,4608]{2,1,0:T(8,128)} %get-tuple-element.58), channel_id=1, source_target_pairs={{0,3},{1,2},{2,1},{3,0},{4,7},{5,6},{6,5},{7,4},{8,11},{9,10},{10,... | collective-permute-start | bytes 442376 | tf_op jit(solution)/shard_map/ppermute | solution.py:56
  48.4 10.1 %copy-start.1 = (bf16[2,1,32,4608]{3,2,1,0:T(8,128)(2,1)S(1)}, bf16[2,1,32,4608]{3,2,1,0:T(8,128)(2,1)}, u32[]{:S(2)}) copy-start(bf16[2,1,32,4608]{3,2,1,0:T(8,128)(2,1)} %param.13) | copy-start | bytes 1769476
  52.8 15.8 %all-to-all-start.1 = ((bf16[8,2,9216]{2,1,0:T(2,128)(2,1)}), bf16[8,2,9216]{2,1,0:T(2,128)(2,1)S(1)}, u32[]{:S(2)}, u32[]{:S(2)}) async-start(bf16[8,2,9216]{2,1,0:T(2,128)(2,1)} %reshape.50), calls=%async_computation.1 | async-start | bytes 589824 | tf_op jit(solution)/shard_map/all_to_all | solution.py:69
  68.6 19.6 %all-to-all-start = ((bf16[2,1,32,4608]{3,0,1,2:T(2,128)(2,1)}), bf16[2,1,32,4608]{3,0,1,2:T(2,128)(2,1)S(1)}, u32[]{:S(2)}, u32[]{:S(2)}) async-start(bf16[2,1,32,4608]{3,0,1,2:T(2,128)(2,1)} %copy.14), calls=%async_computation | async-start | bytes 1179648 | tf_op jit(solution)/shard_map/all_to_all | solution.py:38
